TPU v7x, 32 devices: a whole 2x2x4 slice. The times are simulated.
32 devices in a mesh: batch: 16 (over z, x, core), rep: 2 (over y).
Axes of the slice: x: 2, y: 2, z: 4, core: 2. Of those that a mesh axis runs over, the one named last changes fastest.
Arguments:
- behav_ids: int32 [512, 256], P(('batch', 'rep')), may hold values from 0 to 1023
- lengths: int32 [512], P(('batch', 'rep')), may hold values from 32 to 256
- cand_ids: int32 [512, 16], P(('batch', 'rep')), may hold values from 0 to 1023
- labels: int32 [512, 16], P(('batch', 'rep')), may hold values 0 or 1
- item_table: float32 [1024, 128], replicated, may hold values from -6 to 6
- att_behav: float32 [128, 80], replicated, may hold values from -0.5 to 0.5
- att_cand: float32 [128, 80], replicated, may hold values from -0.5 to 0.5
- att_bias: float32 [80], replicated, may hold values from -3 to 3
- att_out: float32 [80], replicated, may hold values from -0.625 to 0.625
- dense_in: float32 [512, 256], replicated, may hold values from -0.25 to 0.25
- dense_bias: float32 [256], replicated, may hold values from -3 to 3
- dense_out: float32 [256], replicated, may hold values from -0.375 to 0.375
Outputs:
- grad_table: float32 [1024, 128], replicated
- grad_att_behav: float32 [128, 80], replicated
- grad_att_cand: float32 [128, 80], replicated
- grad_att_bias: float32 [80], replicated
- grad_att_out: float32 [80], replicated
- grad_dense_in: float32 [512, 256], replicated
- grad_dense_bias: float32 [256], replicated
- grad_dense_out: float32 [256], replicated
- mean_loss: float32 [], replicated
All inputs are finite; a program needn't handle non-finite values. No bound on the sum of `labels` on one device may be relied on, other than what follows from the above.
Results may differ from a plain program's by a relative error of at most 0.0003.
Values sent between devices are 32-bit elements; how exact they have to be, the bound alone decides.
No kernel may reach another device: no remote copies, remote signals or barrier semaphores. Data moves between devices by JAX's collectives and lax.ppermute only.
A program may use at most 64 MiB of HBM per device.

v0:
```python
import math
import jax
import jax.numpy as jnp
from jax import lax
from jax.sharding import PartitionSpec as P

SEQ = 256
highest = lax.Precision.HIGHEST


def block_loss(
    item_table,
    att_behav,
    att_cand,
    att_bias,
    att_out,
    dense_in,
    dense_bias,
    dense_out,
    ids_block,
    lens_block,
    cands_block,
    labels_block,
):
    behaviors = item_table[ids_block]
    candidates = item_table[cands_block]
    places = jnp.arange(ids_block.shape[1], dtype=jnp.int32)
    live = (places[None, :] < lens_block[:, None]).astype(jnp.float32)
    pre_behav = jnp.einsum("bse,eh->bsh", behaviors, att_behav, precision=highest)
    pre_cand = jnp.einsum("bpe,eh->bph", candidates, att_cand, precision=highest) + att_bias
    activity = jax.nn.silu(pre_behav[:, None, :, :] + pre_cand[:, :, None, :])
    scores = jnp.einsum("bpsh,h->bps", activity, att_out, precision=highest) * live[:, None, :]
    pooled = jnp.einsum("bps,bse->bpe", scores, behaviors, precision=highest) / SEQ
    average = (
        jnp.einsum("bs,bse->be", live, behaviors, precision=highest)
        / lens_block.astype(jnp.float32)[:, None]
    )
    average = jnp.broadcast_to(average[:, None, :], pooled.shape)
    feature = jnp.concatenate([pooled, candidates, pooled * candidates, average], axis=-1)
    hidden = jax.nn.silu(
        jnp.einsum("bpf,fk->bpk", feature, dense_in, precision=highest) + dense_bias
    )
    logits = jnp.einsum("bpk,k->bp", hidden, dense_out, precision=highest)
    targets = labels_block.astype(jnp.float32)
    return jnp.sum(jax.nn.softplus(logits) - targets * logits)


def body(
    behav_ids,
    lengths,
    cand_ids,
    labels,
    item_table,
    att_behav,
    att_cand,
    att_bias,
    att_out,
    dense_in,
    dense_bias,
    dense_out,
):
    params = (item_table, att_behav, att_cand, att_bias, att_out, dense_in, dense_bias, dense_out)
    users = behav_ids.shape[0]
    group = math.gcd(users, 4)
    ids_blocks = behav_ids.reshape(users // group, group, behav_ids.shape[1])
    lens_blocks = lengths.reshape(users // group, group)
    cands_blocks = cand_ids.reshape(users // group, group, cand_ids.shape[1])
    labels_blocks = labels.reshape(users // group, group, labels.shape[1])

    def accumulate(carry, block):
        ids_block, lens_block, cands_block, labels_block = block

        def closed(*weights):
            return block_loss(*weights, ids_block, lens_block, cands_block, labels_block)

        value, pullback = jax.vjp(closed, *params)
        grads = pullback(jnp.ones_like(value))
        totals = jax.tree.map(lambda left, right: left + right, carry[1], grads)
        return ((carry[0] + value, totals), None)

    start = (jnp.zeros((), jnp.float32), tuple((jnp.zeros_like(weight) for weight in params)))
    (loss_local, grad_local), _ = lax.scan(
        accumulate, start, (ids_blocks, lens_blocks, cands_blocks, labels_blocks)
    )
    pieces = [grad.reshape(-1) for grad in grad_local]
    loss_total = lax.psum(loss_local, ("batch", "rep"))
    flat = jnp.concatenate(pieces)
    summed = lax.psum(flat, ("batch", "rep"))
    count = jnp.float32(users * lax.axis_size("batch") * lax.axis_size("rep") * cand_ids.shape[1])
    results = []
    offset = 0
    for weight in params:
        extent = weight.size
        results.append(summed[offset : offset + extent].reshape(weight.shape) / count)
        offset = offset + extent
    mean_loss = loss_total / count
    return (
        results[0],
        results[1],
        results[2],
        results[3],
        results[4],
        results[5],
        results[6],
        results[7],
        mean_loss,
    )


def solution(mesh):
    placed = (
        P(("batch", "rep"), None),
        P(("batch", "rep")),
        P(("batch", "rep"), None),
        P(("batch", "rep"), None),
        P(),
        P(),
        P(),
        P(),
        P(),
        P(),
        P(),
        P(),
    )
    return jax.shard_map(
        body,
        mesh=mesh,
        in_specs=placed,
        out_specs=(P(), P(), P(), P(), P(), P(), P(), P(), P()),
        check_vma=False,
    )
```

profile of v0, /device:TPU:0, one launch (start us, length us, event | category | flops | bytes accessed | tf_op | source)
XLA Modules:
  0.0 320.4 jit_solution(10956114307714562897)
XLA Ops:
  7.3 0.7 reshape.159
  8.0 0.7 reshape.157
  8.8 150.1 %while.27 = (s32[]{:T(128)}, f32[]{:T(128)}, f32[1024,128]{1,0:T(8,128)S(1)}, f32[128,80]{0,1:T(8,128)S(1)}, f32[128,80]{0,1:T(8,128)S(1)}, /*index=5*/f32[80]{0...) while((s32[]{:T(128)}, f32[]{:T(128)}, ...), condition=%wide.region_9.10_spmd.clone, body=%wide.region_0.9_spmd.clone.sunk | while | flops 845604608 | bytes 17579108 | solution.py:82
  9.7 1.6 gather_fusion.1
  11.3 1.0 convolution_add_fusion.10
  12.3 3.9 %gather_fusion = f32[1024,128]{1,0:T(8,128)S(1)} fusion(f32[1024,128]{1,0:T(8,128)} %get-tuple-element.510, s32[1024]{0:T(1024)S(1)} %broadcast_clamp_fusion.2), kind=kCustom, calls=%fused_computation.clone.clone.1 | custom fusion | bytes 1052672 | tf_op jit(solution)/shard_map/while/body/eval_jaxpr/jvp()/gather | solution.py:25
  16.5 0.7 fusion.167
  17.3 3.9 %fusion.168 = f32[1,4,16,256]{3,0,2,1:T(1,128)S(1)} fusion(f32[4,16,80]{2,1,0:T(8,128)S(1)} %convolution_add_fusion.10, f32[4,256,80]{1,2,0:T(8,128)S(1)} %fusion.167, f32[80]{0:T(128)S(1)} %copy-done.5), kind=kOutput, calls=%fused_computation.15.clone.1 | convolution fusion | flops 22282240 | bytes 414016 | tf_op jit(solution)/shard_map/while/body/eval_jaxpr/jvp(bpsh,h->bps)/dot_general | solution.py:32
  22.3 1.3 fusion.171
  25.9 4.7 %fusion.177 = f32[80]{0:T(128)S(1)} fusion(f32[4,16,80]{2,1,0:T(8,128)S(1)} %convolution_add_fusion.10, f32[4,256,80]{1,2,0:T(8,128)S(1)} %fusion.167, f32[4,16,256,1]{2,1,0,3:T(8,128)S(1)} %bitcast.199, f32[80]{0:T(128)S(1)} %get-tuple-element.480, pred[]{:T(512)S(6)} %compare.3), kind=kOutput, calls=%fused_computation.37.clone.1 | convolution fusion | flops 22282400 | bytes 414337 | tf_op jit(solution)/shard_map/while/body/eval_jaxpr/transpose(jvp(bpsh,h->bps))/dot_general | solution.py:32
  30.6 4.3 %fusion.173 = (f32[80]{0:T(128)S(1)}, f32[4,256,80]{1,2,0:T(8,128)S(1)}, f32[4,16,80]{2,1,0:T(8,128)S(1)}) fusion(f32[4,16,80]{2,1,0:T(8,128)S(1)} %convolution_add_fusion.10, f32[4,256,80]{1,2,0:T(8,128)S(1)} %fusion.167, f32[80]{0:T(128)S(1)} %copy-done.5, f32[4,16,256]{2,1,0:T(8,128)S(1)} %convolution_multiply_fusion.3), kind=kLoop, calls=%fused_computation.20.clone.1 | loop fusion | flops 18262960 | bytes 762496 | tf_op jit(solution)/shard_map/while/body/eval_jaxpr/transpose(jvp())/reduce_sum | solution.py:30
  35.8 1.1 convolution_add_fusion.13
  37.0 1.0 convolution_add_fusion.14
  38.0 6.1 %scatter_custom_fusion.13 = f32[1024,128]{1,0:T(8,128)S(1)} fusion(s32[1024]{0:T(1024)S(1)} %bitcast.204, f32[1024,128]{1,0:T(8,128)S(1)} %bitcast.197, f32[]{:T(128)} %constant.34.clone.1..sunk), kind=kCustom, calls=%fused_computation.42.clone.1 | custom fusion | flops 131072 | bytes 524292 | tf_op jit(solution)/shard_map/while/body/eval_jaxpr/transpose(jvp())/scatter-add | solution.py:25
  44.1 0.9 fusion.178
  45.0 0.9 scatter_custom_fusion.12
  47.2 1.6 gather_fusion.1
  48.8 1.0 convolution_add_fusion.10
  49.8 3.9 %gather_fusion = f32[1024,128]{1,0:T(8,128)S(1)} fusion(f32[1024,128]{1,0:T(8,128)} %get-tuple-element.510, s32[1024]{0:T(1024)S(1)} %broadcast_clamp_fusion.2), kind=kCustom, calls=%fused_computation.clone.clone.1 | custom fusion | bytes 1052672 | tf_op jit(solution)/shard_map/while/body/eval_jaxpr/jvp()/gather | solution.py:25
  54.1 0.7 fusion.167
  54.8 3.9 %fusion.168 = f32[1,4,16,256]{3,0,2,1:T(1,128)S(1)} fusion(f32[4,16,80]{2,1,0:T(8,128)S(1)} %convolution_add_fusion.10, f32[4,256,80]{1,2,0:T(8,128)S(1)} %fusion.167, f32[80]{0:T(128)S(1)} %copy-done.5), kind=kOutput, calls=%fused_computation.15.clone.1 | convolution fusion | flops 22282240 | bytes 414016 | tf_op jit(solution)/shard_map/while/body/eval_jaxpr/jvp(bpsh,h->bps)/dot_general | solution.py:32
  59.9 1.3 fusion.171
  63.4 4.7 %fusion.177 = f32[80]{0:T(128)S(1)} fusion(f32[4,16,80]{2,1,0:T(8,128)S(1)} %convolution_add_fusion.10, f32[4,256,80]{1,2,0:T(8,128)S(1)} %fusion.167, f32[4,16,256,1]{2,1,0,3:T(8,128)S(1)} %bitcast.199, f32[80]{0:T(128)S(1)} %get-tuple-element.480, pred[]{:T(512)S(6)} %compare.3), kind=kOutput, calls=%fused_computation.37.clone.1 | convolution fusion | flops 22282400 | bytes 414337 | tf_op jit(solution)/shard_map/while/body/eval_jaxpr/transpose(jvp(bpsh,h->bps))/dot_general | solution.py:32
  68.1 4.3 %fusion.173 = (f32[80]{0:T(128)S(1)}, f32[4,256,80]{1,2,0:T(8,128)S(1)}, f32[4,16,80]{2,1,0:T(8,128)S(1)}) fusion(f32[4,16,80]{2,1,0:T(8,128)S(1)} %convolution_add_fusion.10, f32[4,256,80]{1,2,0:T(8,128)S(1)} %fusion.167, f32[80]{0:T(128)S(1)} %copy-done.5, f32[4,16,256]{2,1,0:T(8,128)S(1)} %convolution_multiply_fusion.3), kind=kLoop, calls=%fused_computation.20.clone.1 | loop fusion | flops 18262960 | bytes 762496 | tf_op jit(solution)/shard_map/while/body/eval_jaxpr/transpose(jvp())/reduce_sum | solution.py:30
  73.4 1.1 convolution_add_fusion.13
  74.5 1.0 convolution_add_fusion.14
  75.5 6.1 %scatter_custom_fusion.13 = f32[1024,128]{1,0:T(8,128)S(1)} fusion(s32[1024]{0:T(1024)S(1)} %bitcast.204, f32[1024,128]{1,0:T(8,128)S(1)} %bitcast.197, f32[]{:T(128)} %constant.34.clone.1..sunk), kind=kCustom, calls=%fused_computation.42.clone.1 | custom fusion | flops 131072 | bytes 524292 | tf_op jit(solution)/shard_map/while/body/eval_jaxpr/transpose(jvp())/scatter-add | solution.py:25
  81.7 0.9 fusion.178
  82.5 0.9 scatter_custom_fusion.12
  84.7 1.6 gather_fusion.1
  86.4 1.0 convolution_add_fusion.10
  87.4 3.9 %gather_fusion = f32[1024,128]{1,0:T(8,128)S(1)} fusion(f32[1024,128]{1,0:T(8,128)} %get-tuple-element.510, s32[1024]{0:T(1024)S(1)} %broadcast_clamp_fusion.2), kind=kCustom, calls=%fused_computation.clone.clone.1 | custom fusion | bytes 1052672 | tf_op jit(solution)/shard_map/while/body/eval_jaxpr/jvp()/gather | solution.py:25
  91.6 0.7 fusion.167
  92.4 3.9 %fusion.168 = f32[1,4,16,256]{3,0,2,1:T(1,128)S(1)} fusion(f32[4,16,80]{2,1,0:T(8,128)S(1)} %convolution_add_fusion.10, f32[4,256,80]{1,2,0:T(8,128)S(1)} %fusion.167, f32[80]{0:T(128)S(1)} %copy-done.5), kind=kOutput, calls=%fused_computation.15.clone.1 | convolution fusion | flops 22282240 | bytes 414016 | tf_op jit(solution)/shard_map/while/body/eval_jaxpr/jvp(bpsh,h->bps)/dot_general | solution.py:32
  97.4 1.3 fusion.171
  101.0 4.7 %fusion.177 = f32[80]{0:T(128)S(1)} fusion(f32[4,16,80]{2,1,0:T(8,128)S(1)} %convolution_add_fusion.10, f32[4,256,80]{1,2,0:T(8,128)S(1)} %fusion.167, f32[4,16,256,1]{2,1,0,3:T(8,128)S(1)} %bitcast.199, f32[80]{0:T(128)S(1)} %get-tuple-element.480, pred[]{:T(512)S(6)} %compare.3), kind=kOutput, calls=%fused_computation.37.clone.1 | convolution fusion | flops 22282400 | bytes 414337 | tf_op jit(solution)/shard_map/while/body/eval_jaxpr/transpose(jvp(bpsh,h->bps))/dot_general | solution.py:32
  105.7 4.3 %fusion.173 = (f32[80]{0:T(128)S(1)}, f32[4,256,80]{1,2,0:T(8,128)S(1)}, f32[4,16,80]{2,1,0:T(8,128)S(1)}) fusion(f32[4,16,80]{2,1,0:T(8,128)S(1)} %convolution_add_fusion.10, f32[4,256,80]{1,2,0:T(8,128)S(1)} %fusion.167, f32[80]{0:T(128)S(1)} %copy-done.5, f32[4,16,256]{2,1,0:T(8,128)S(1)} %convolution_multiply_fusion.3), kind=kLoop, calls=%fused_computation.20.clone.1 | loop fusion | flops 18262960 | bytes 762496 | tf_op jit(solution)/shard_map/while/body/eval_jaxpr/transpose(jvp())/reduce_sum | solution.py:30
  110.9 1.1 convolution_add_fusion.13
  112.0 1.0 convolution_add_fusion.14
  113.0 6.1 %scatter_custom_fusion.13 = f32[1024,128]{1,0:T(8,128)S(1)} fusion(s32[1024]{0:T(1024)S(1)} %bitcast.204, f32[1024,128]{1,0:T(8,128)S(1)} %bitcast.197, f32[]{:T(128)} %constant.34.clone.1..sunk), kind=kCustom, calls=%fused_computation.42.clone.1 | custom fusion | flops 131072 | bytes 524292 | tf_op jit(solution)/shard_map/while/body/eval_jaxpr/transpose(jvp())/scatter-add | solution.py:25
  119.2 0.9 fusion.178
  120.1 0.9 scatter_custom_fusion.12
  122.3 1.6 gather_fusion.1
  123.9 1.0 convolution_add_fusion.10
  124.9 3.9 %gather_fusion = f32[1024,128]{1,0:T(8,128)S(1)} fusion(f32[1024,128]{1,0:T(8,128)} %get-tuple-element.510, s32[1024]{0:T(1024)S(1)} %broadcast_clamp_fusion.2), kind=kCustom, calls=%fused_computation.clone.clone.1 | custom fusion | bytes 1052672 | tf_op jit(solution)/shard_map/while/body/eval_jaxpr/jvp()/gather | solution.py:25
  129.9 3.9 %fusion.168 = f32[1,4,16,256]{3,0,2,1:T(1,128)S(1)} fusion(f32[4,16,80]{2,1,0:T(8,128)S(1)} %convolution_add_fusion.10, f32[4,256,80]{1,2,0:T(8,128)S(1)} %fusion.167, f32[80]{0:T(128)S(1)} %copy-done.5), kind=kOutput, calls=%fused_computation.15.clone.1 | convolution fusion | flops 22282240 | bytes 414016 | tf_op jit(solution)/shard_map/while/body/eval_jaxpr/jvp(bpsh,h->bps)/dot_general | solution.py:32
  135.0 1.3 fusion.171
  138.5 4.7 %fusion.177 = f32[80]{0:T(128)S(1)} fusion(f32[4,16,80]{2,1,0:T(8,128)S(1)} %convolution_add_fusion.10, f32[4,256,80]{1,2,0:T(8,128)S(1)} %fusion.167, f32[4,16,256,1]{2,1,0,3:T(8,128)S(1)} %bitcast.199, f32[80]{0:T(128)S(1)} %get-tuple-element.480, pred[]{:T(512)S(6)} %compare.3), kind=kOutput, calls=%fused_computation.37.clone.1 | convolution fusion | flops 22282400 | bytes 414337 | tf_op jit(solution)/shard_map/while/body/eval_jaxpr/transpose(jvp(bpsh,h->bps))/dot_general | solution.py:32
  143.2 4.3 %fusion.173 = (f32[80]{0:T(128)S(1)}, f32[4,256,80]{1,2,0:T(8,128)S(1)}, f32[4,16,80]{2,1,0:T(8,128)S(1)}) fusion(f32[4,16,80]{2,1,0:T(8,128)S(1)} %convolution_add_fusion.10, f32[4,256,80]{1,2,0:T(8,128)S(1)} %fusion.167, f32[80]{0:T(128)S(1)} %copy-done.5, f32[4,16,256]{2,1,0:T(8,128)S(1)} %convolution_multiply_fusion.3), kind=kLoop, calls=%fused_computation.20.clone.1 | loop fusion | flops 18262960 | bytes 762496 | tf_op jit(solution)/shard_map/while/body/eval_jaxpr/transpose(jvp())/reduce_sum | solution.py:30
  148.5 1.1 convolution_add_fusion.13
  149.6 1.0 convolution_add_fusion.14
  150.6 6.1 %scatter_custom_fusion.13 = f32[1024,128]{1,0:T(8,128)S(1)} fusion(s32[1024]{0:T(1024)S(1)} %bitcast.204, f32[1024,128]{1,0:T(8,128)S(1)} %bitcast.197, f32[]{:T(128)} %constant.34.clone.1..sunk), kind=kCustom, calls=%fused_computation.42.clone.1 | custom fusion | flops 131072 | bytes 524292 | tf_op jit(solution)/shard_map/while/body/eval_jaxpr/transpose(jvp())/scatter-add | solution.py:25
  156.7 0.9 fusion.178
  157.6 0.9 scatter_custom_fusion.12
  159.6 10.3 %concatenate.6 = f32[283296]{0:T(1024)} concatenate(f32[131072]{0:T(1024)S(1)} %bitcast.196, f32[10240]{0:T(1024)S(1)} %reshape.162, f32[10240]{0:T(1024)S(1)} %reshape.163, f32[80]{0:T(128)S(1)} %get-tuple-element.132, f32[80]{0:T(128)S(1)} %get-tuple-element.133, f32[131072]{0:T(1024)S(1)} %bitcast.198, f32[256]{0:T(256)S(1)} %get-tuple-element.135, f32[256]{0:T(256)S(1)} %get-tuple-element.136), dimensions={0} | concatenate | bytes 2266368 | tf_op jit(solution)/shard_map/concatenate | solution.py:87
  169.9 42.8 %psum.15 = f32[]{:T(128)} all-reduce(f32[]{:T(128)} %get-tuple-element.137), channel_id=1, replica_groups=mesh['batch'=16,'rep'=2] {'batch','rep'}, use_global_device_ids=true, to_apply=%region_11.12 | all-reduce | flops 1 | bytes 8 | tf_op jit(solution)/shard_map/psum | solution.py:86
  213.4 90.8 %all-reduce.2.cloned.1.call-done = f32[283296]{0:T(1024)} async-done(((f32[283296]{0:T(1024)}), f32[283296]{0:T(1024)}) %all-reduce.2.cloned.1.call-update) | async-done | bytes 1133200 | tf_op jit(solution)/shard_map/psum | solution.py:88
  304.2 2.2 slice_multiply_fusion
  306.4 0.9 div.77
  307.3 0.8 slice_multiply_fusion.2
  308.2 0.7 copy.30
  309.0 0.7 copy.29
  309.7 1.3 slice_multiply_fusion.6
  311.0 1.4 slice_multiply_fusion.4
  (170 shorter events, 22.6 us)
Async XLA Ops:
  7.2 297.0 %all-reduce.2.cloned.1.call-start = ((), (), s32[]{:S(2)}) async-start(), calls=%async_computation | async-start | bytes 2269184 | tf_op jit(solution)/shard_map/psum | solution.py:88
  12.3 4.3 %copy-start.1 = (f32[128,80]{0,1:T(8,128)S(1)}, f32[128,80]{0,1:T(8,128)}, u32[]{:S(2)}) copy-start(f32[128,80]{0,1:T(8,128)} %get-tuple-element.511) | copy-start | bytes 122884 | tf_op jit(solution)/shard_map/while
  16.2 1.1 copy-start.5
  17.2 4.3 %copy-start = (f32[512,256]{1,0:T(8,128)S(1)}, f32[512,256]{1,0:T(8,128)}, u32[]{:S(2)}) copy-start(f32[512,256]{1,0:T(8,128)} %get-tuple-element.517) | copy-start | bytes 1572868 | tf_op jit(solution)/shard_map/while
  17.3 4.3 %copy-start.4 = (f32[256]{0:T(256)S(1)}, f32[256]{0:T(256)}, u32[]{:S(2)}) copy-start(f32[256]{0:T(256)} %get-tuple-element.518) | copy-start | bytes 3076 | tf_op jit(solution)/shard_map/while
  21.2 0.8 copy-start.3
  30.6 4.8 %copy-start.2 = (f32[128,80]{0,1:T(8,128)S(1)}, f32[128,80]{0,1:T(8,128)}, u32[]{:S(2)}) copy-start(f32[128,80]{0,1:T(8,128)} %get-tuple-element.513) | copy-start | bytes 122884 | tf_op jit(solution)/shard_map/while
  49.8 4.3 %copy-start.1 = (f32[128,80]{0,1:T(8,128)S(1)}, f32[128,80]{0,1:T(8,128)}, u32[]{:S(2)}) copy-start(f32[128,80]{0,1:T(8,128)} %get-tuple-element.511) | copy-start | bytes 122884 | tf_op jit(solution)/shard_map/while
  53.7 1.1 copy-start.5
  54.8 4.3 %copy-start = (f32[512,256]{1,0:T(8,128)S(1)}, f32[512,256]{1,0:T(8,128)}, u32[]{:S(2)}) copy-start(f32[512,256]{1,0:T(8,128)} %get-tuple-element.517) | copy-start | bytes 1572868 | tf_op jit(solution)/shard_map/while
  54.8 4.3 %copy-start.4 = (f32[256]{0:T(256)S(1)}, f32[256]{0:T(256)}, u32[]{:S(2)}) copy-start(f32[256]{0:T(256)} %get-tuple-element.518) | copy-start | bytes 3076 | tf_op jit(solution)/shard_map/while
  58.7 0.8 copy-start.3
  68.1 4.8 %copy-start.2 = (f32[128,80]{0,1:T(8,128)S(1)}, f32[128,80]{0,1:T(8,128)}, u32[]{:S(2)}) copy-start(f32[128,80]{0,1:T(8,128)} %get-tuple-element.513) | copy-start | bytes 122884 | tf_op jit(solution)/shard_map/while
  87.4 4.3 %copy-start.1 = (f32[128,80]{0,1:T(8,128)S(1)}, f32[128,80]{0,1:T(8,128)}, u32[]{:S(2)}) copy-start(f32[128,80]{0,1:T(8,128)} %get-tuple-element.511) | copy-start | bytes 122884 | tf_op jit(solution)/shard_map/while
  91.2 1.1 copy-start.5
  92.3 4.3 %copy-start = (f32[512,256]{1,0:T(8,128)S(1)}, f32[512,256]{1,0:T(8,128)}, u32[]{:S(2)}) copy-start(f32[512,256]{1,0:T(8,128)} %get-tuple-element.517) | copy-start | bytes 1572868 | tf_op jit(solution)/shard_map/while
  92.3 4.3 %copy-start.4 = (f32[256]{0:T(256)S(1)}, f32[256]{0:T(256)}, u32[]{:S(2)}) copy-start(f32[256]{0:T(256)} %get-tuple-element.518) | copy-start | bytes 3076 | tf_op jit(solution)/shard_map/while
  96.3 0.8 copy-start.3
  105.6 4.8 %copy-start.2 = (f32[128,80]{0,1:T(8,128)S(1)}, f32[128,80]{0,1:T(8,128)}, u32[]{:S(2)}) copy-start(f32[128,80]{0,1:T(8,128)} %get-tuple-element.513) | copy-start | bytes 122884 | tf_op jit(solution)/shard_map/while
  124.9 4.3 %copy-start.1 = (f32[128,80]{0,1:T(8,128)S(1)}, f32[128,80]{0,1:T(8,128)}, u32[]{:S(2)}) copy-start(f32[128,80]{0,1:T(8,128)} %get-tuple-element.511) | copy-start | bytes 122884 | tf_op jit(solution)/shard_map/while
  128.8 1.1 copy-start.5
  129.9 4.3 %copy-start = (f32[512,256]{1,0:T(8,128)S(1)}, f32[512,256]{1,0:T(8,128)}, u32[]{:S(2)}) copy-start(f32[512,256]{1,0:T(8,128)} %get-tuple-element.517) | copy-start | bytes 1572868 | tf_op jit(solution)/shard_map/while
  129.9 4.3 %copy-start.4 = (f32[256]{0:T(256)S(1)}, f32[256]{0:T(256)}, u32[]{:S(2)}) copy-start(f32[256]{0:T(256)} %get-tuple-element.518) | copy-start | bytes 3076 | tf_op jit(solution)/shard_map/while
  133.8 0.8 copy-start.3
  143.2 4.8 %copy-start.2 = (f32[128,80]{0,1:T(8,128)S(1)}, f32[128,80]{0,1:T(8,128)}, u32[]{:S(2)}) copy-start(f32[128,80]{0,1:T(8,128)} %get-tuple-element.513) | copy-start | bytes 122884 | tf_op jit(solution)/shard_map/while
Sparse Core Ops, SparseCore 0:
  170.1 134.0 all-reduce.1
where the time goes:
time: 322 us; the launch traced here: 320 us
  waiting for transfers between devices  90.8 us (28%)
  matrix products  67.7 us (21%)
  other arithmetic  62 us (19%)
  blocking collectives  42.8 us (13%)
  local copies, waits for them, and re-layouts  37.5 us (12%)
  between operations  15.9 us (5%)
  loops' own time  3.61 us (1%)
    psum x1, waiting for transfers between devices, body(): summed = lax.psum(flat, ('batch', 'rep'))  90.8 us
    psum x1, blocking collectives, body(): loss_total = lax.psum(loss_local, ('batch', 'rep'))  42.8 us
    dot_general x8, matrix products, block_loss(): jnp.einsum('bpsh,h->bps', activity, att_out, precision=highest)  34.2 us
    scatter-add x4, other arithmetic, block_loss(): behaviors = item_table[ids_block]  24.6 us
    reduce_sum x4, other arithmetic, block_loss(): jnp.einsum('bpe,eh->bph', candidates, att_cand, precision=highest)  17 us
    gather x4, local copies, waits for them, and re-layouts, block_loss(): behaviors = item_table[ids_block]  15.4 us
    concatenate x1, local copies, waits for them, and re-layouts, body(): flat = jnp.concatenate(pieces)  10.3 us
    dot_general x12, matrix products, block_loss(): jnp.einsum('bse,eh->bsh', behaviors, att_behav, precision=highest)  8.88 us
  transfers between devices with their start and end apart: 1, of which 1 were waited for; matrix products, arithmetic and copies ran while one was open for 0% of the time, Pallas kernels for 0%

commit v1 on v0

--- a/solution.py
+++ b/solution.py
@@ -85,7 +85,7 @@
     pieces = [grad.reshape(-1) for grad in grad_local]
     loss_total = lax.psum(loss_local, ("batch", "rep"))
     flat = jnp.concatenate(pieces)
-    summed = lax.psum(flat, ("batch", "rep"))
+    summed = lax.psum(lax.psum(flat, "batch"), "rep")
     count = jnp.float32(users * lax.axis_size("batch") * lax.axis_size("rep") * cand_ids.shape[1])
     results = []
     offset = 0

time: 322 us -> 328 us (1.019)
  waiting for transfers between devices: 90.8 us -> 98.6 us
    psum x1 -> x2, waiting for transfers between devices: 90.8 us -> 98.6 us  [body(): summed = lax.psum(lax.psum(flat, 'batch'), 'rep')]
  transfers between devices with their start and end apart: 1 -> 2, of which waited for: 1 -> 2; matrix products, arithmetic and copies ran while one was open for 0% -> 0% of each run, Pallas kernels for 0% -> 0%
where the time goes in v1:
time: 328 us; the launch traced here: 327 us
  waiting for transfers between devices  98.6 us (30%)
  matrix products  67.7 us (21%)
  other arithmetic  62 us (19%)
  blocking collectives  41.6 us (13%)
  local copies, waits for them, and re-layouts  37.5 us (11%)
  between operations  16 us (5%)
  loops' own time  3.61 us (1%)
    psum x2, waiting for transfers between devices, body(): summed = lax.psum(lax.psum(flat, 'batch'), 'rep')  98.6 us
    psum x1, blocking collectives, body(): loss_total = lax.psum(loss_local, ('batch', 'rep'))  41.6 us
    dot_general x8, matrix products, block_loss(): jnp.einsum('bpsh,h->bps', activity, att_out, precision=highest)  34.2 us
    scatter-add x4, other arithmetic, block_loss(): behaviors = item_table[ids_block]  24.6 us
    reduce_sum x4, other arithmetic, block_loss(): jnp.einsum('bpe,eh->bph', candidates, att_cand, precision=highest)  17 us
    gather x4, local copies, waits for them, and re-layouts, block_loss(): behaviors = item_table[ids_block]  15.4 us
    concatenate x1, local copies, waits for them, and re-layouts, body(): flat = jnp.concatenate(pieces)  10.3 us
    dot_general x12, matrix products, block_loss(): jnp.einsum('bse,eh->bsh', behaviors, att_behav, precision=highest)  8.88 us
  transfers between devices with their start and end apart: 2, of which 2 were waited for; matrix products, arithmetic and copies ran while one was open for 0% of the time, Pallas kernels for 0%

profile of v1, /device:TPU:0, one launch (start us, length us, event | category | flops | bytes accessed | tf_op | source)
XLA Modules:
  0.0 327.1 jit_solution(3144539896731183538)
XLA Ops:
  7.3 0.7 reshape.159
  8.0 0.7 reshape.157
  8.8 150.1 %while.27 = (s32[]{:T(128)}, f32[]{:T(128)}, f32[1024,128]{1,0:T(8,128)S(1)}, f32[128,80]{0,1:T(8,128)S(1)}, f32[128,80]{0,1:T(8,128)S(1)}, /*index=5*/f32[80]{0...) while((s32[]{:T(128)}, f32[]{:T(128)}, ...), condition=%wide.region_9.10_spmd.clone, body=%wide.region_0.9_spmd.clone.sunk | while | flops 845604608 | bytes 17579108 | solution.py:82
  9.7 1.6 gather_fusion.1
  11.3 1.0 convolution_add_fusion.10
  12.3 3.9 %gather_fusion = f32[1024,128]{1,0:T(8,128)S(1)} fusion(f32[1024,128]{1,0:T(8,128)} %get-tuple-element.510, s32[1024]{0:T(1024)S(1)} %broadcast_clamp_fusion.2), kind=kCustom, calls=%fused_computation.clone.clone.1 | custom fusion | bytes 1052672 | tf_op jit(solution)/shard_map/while/body/eval_jaxpr/jvp()/gather | solution.py:25
  16.5 0.7 fusion.167
  17.3 3.9 %fusion.168 = f32[1,4,16,256]{3,0,2,1:T(1,128)S(1)} fusion(f32[4,16,80]{2,1,0:T(8,128)S(1)} %convolution_add_fusion.10, f32[4,256,80]{1,2,0:T(8,128)S(1)} %fusion.167, f32[80]{0:T(128)S(1)} %copy-done.5), kind=kOutput, calls=%fused_computation.15.clone.1 | convolution fusion | flops 22282240 | bytes 414016 | tf_op jit(solution)/shard_map/while/body/eval_jaxpr/jvp(bpsh,h->bps)/dot_general | solution.py:32
  22.3 1.3 fusion.171
  25.9 4.7 %fusion.177 = f32[80]{0:T(128)S(1)} fusion(f32[4,16,80]{2,1,0:T(8,128)S(1)} %convolution_add_fusion.10, f32[4,256,80]{1,2,0:T(8,128)S(1)} %fusion.167, f32[4,16,256,1]{2,1,0,3:T(8,128)S(1)} %bitcast.199, f32[80]{0:T(128)S(1)} %get-tuple-element.480, pred[]{:T(512)S(6)} %compare.3), kind=kOutput, calls=%fused_computation.37.clone.1 | convolution fusion | flops 22282400 | bytes 414337 | tf_op jit(solution)/shard_map/while/body/eval_jaxpr/transpose(jvp(bpsh,h->bps))/dot_general | solution.py:32
  30.6 4.3 %fusion.173 = (f32[80]{0:T(128)S(1)}, f32[4,256,80]{1,2,0:T(8,128)S(1)}, f32[4,16,80]{2,1,0:T(8,128)S(1)}) fusion(f32[4,16,80]{2,1,0:T(8,128)S(1)} %convolution_add_fusion.10, f32[4,256,80]{1,2,0:T(8,128)S(1)} %fusion.167, f32[80]{0:T(128)S(1)} %copy-done.5, f32[4,16,256]{2,1,0:T(8,128)S(1)} %convolution_multiply_fusion.3), kind=kLoop, calls=%fused_computation.20.clone.1 | loop fusion | flops 18262960 | bytes 762496 | tf_op jit(solution)/shard_map/while/body/eval_jaxpr/transpose(jvp())/reduce_sum | solution.py:30
  35.8 1.1 convolution_add_fusion.13
  37.0 1.0 convolution_add_fusion.14
  38.0 6.1 %scatter_custom_fusion.13 = f32[1024,128]{1,0:T(8,128)S(1)} fusion(s32[1024]{0:T(1024)S(1)} %bitcast.204, f32[1024,128]{1,0:T(8,128)S(1)} %bitcast.197, f32[]{:T(128)} %constant.34.clone.1..sunk), kind=kCustom, calls=%fused_computation.42.clone.1 | custom fusion | flops 131072 | bytes 524292 | tf_op jit(solution)/shard_map/while/body/eval_jaxpr/transpose(jvp())/scatter-add | solution.py:25
  44.1 0.9 fusion.178
  45.0 0.9 scatter_custom_fusion.12
  47.2 1.6 gather_fusion.1
  48.8 1.0 convolution_add_fusion.10
  49.8 3.9 %gather_fusion = f32[1024,128]{1,0:T(8,128)S(1)} fusion(f32[1024,128]{1,0:T(8,128)} %get-tuple-element.510, s32[1024]{0:T(1024)S(1)} %broadcast_clamp_fusion.2), kind=kCustom, calls=%fused_computation.clone.clone.1 | custom fusion | bytes 1052672 | tf_op jit(solution)/shard_map/while/body/eval_jaxpr/jvp()/gather | solution.py:25
  54.1 0.7 fusion.167
  54.8 3.9 %fusion.168 = f32[1,4,16,256]{3,0,2,1:T(1,128)S(1)} fusion(f32[4,16,80]{2,1,0:T(8,128)S(1)} %convolution_add_fusion.10, f32[4,256,80]{1,2,0:T(8,128)S(1)} %fusion.167, f32[80]{0:T(128)S(1)} %copy-done.5), kind=kOutput, calls=%fused_computation.15.clone.1 | convolution fusion | flops 22282240 | bytes 414016 | tf_op jit(solution)/shard_map/while/body/eval_jaxpr/jvp(bpsh,h->bps)/dot_general | solution.py:32
  59.9 1.3 fusion.171
  63.4 4.7 %fusion.177 = f32[80]{0:T(128)S(1)} fusion(f32[4,16,80]{2,1,0:T(8,128)S(1)} %convolution_add_fusion.10, f32[4,256,80]{1,2,0:T(8,128)S(1)} %fusion.167, f32[4,16,256,1]{2,1,0,3:T(8,128)S(1)} %bitcast.199, f32[80]{0:T(128)S(1)} %get-tuple-element.480, pred[]{:T(512)S(6)} %compare.3), kind=kOutput, calls=%fused_computation.37.clone.1 | convolution fusion | flops 22282400 | bytes 414337 | tf_op jit(solution)/shard_map/while/body/eval_jaxpr/transpose(jvp(bpsh,h->bps))/dot_general | solution.py:32
  68.1 4.3 %fusion.173 = (f32[80]{0:T(128)S(1)}, f32[4,256,80]{1,2,0:T(8,128)S(1)}, f32[4,16,80]{2,1,0:T(8,128)S(1)}) fusion(f32[4,16,80]{2,1,0:T(8,128)S(1)} %convolution_add_fusion.10, f32[4,256,80]{1,2,0:T(8,128)S(1)} %fusion.167, f32[80]{0:T(128)S(1)} %copy-done.5, f32[4,16,256]{2,1,0:T(8,128)S(1)} %convolution_multiply_fusion.3), kind=kLoop, calls=%fused_computation.20.clone.1 | loop fusion | flops 18262960 | bytes 762496 | tf_op jit(solution)/shard_map/while/body/eval_jaxpr/transpose(jvp())/reduce_sum | solution.py:30
  73.4 1.1 convolution_add_fusion.13
  74.5 1.0 convolution_add_fusion.14
  75.5 6.1 %scatter_custom_fusion.13 = f32[1024,128]{1,0:T(8,128)S(1)} fusion(s32[1024]{0:T(1024)S(1)} %bitcast.204, f32[1024,128]{1,0:T(8,128)S(1)} %bitcast.197, f32[]{:T(128)} %constant.34.clone.1..sunk), kind=kCustom, calls=%fused_computation.42.clone.1 | custom fusion | flops 131072 | bytes 524292 | tf_op jit(solution)/shard_map/while/body/eval_jaxpr/transpose(jvp())/scatter-add | solution.py:25
  81.7 0.9 fusion.178
  82.5 0.9 scatter_custom_fusion.12
  84.7 1.6 gather_fusion.1
  86.4 1.0 convolution_add_fusion.10
  87.4 3.9 %gather_fusion = f32[1024,128]{1,0:T(8,128)S(1)} fusion(f32[1024,128]{1,0:T(8,128)} %get-tuple-element.510, s32[1024]{0:T(1024)S(1)} %broadcast_clamp_fusion.2), kind=kCustom, calls=%fused_computation.clone.clone.1 | custom fusion | bytes 1052672 | tf_op jit(solution)/shard_map/while/body/eval_jaxpr/jvp()/gather | solution.py:25
  92.4 3.9 %fusion.168 = f32[1,4,16,256]{3,0,2,1:T(1,128)S(1)} fusion(f32[4,16,80]{2,1,0:T(8,128)S(1)} %convolution_add_fusion.10, f32[4,256,80]{1,2,0:T(8,128)S(1)} %fusion.167, f32[80]{0:T(128)S(1)} %copy-done.5), kind=kOutput, calls=%fused_computation.15.clone.1 | convolution fusion | flops 22282240 | bytes 414016 | tf_op jit(solution)/shard_map/while/body/eval_jaxpr/jvp(bpsh,h->bps)/dot_general | solution.py:32
  97.4 1.3 fusion.171
  101.0 4.7 %fusion.177 = f32[80]{0:T(128)S(1)} fusion(f32[4,16,80]{2,1,0:T(8,128)S(1)} %convolution_add_fusion.10, f32[4,256,80]{1,2,0:T(8,128)S(1)} %fusion.167, f32[4,16,256,1]{2,1,0,3:T(8,128)S(1)} %bitcast.199, f32[80]{0:T(128)S(1)} %get-tuple-element.480, pred[]{:T(512)S(6)} %compare.3), kind=kOutput, calls=%fused_computation.37.clone.1 | convolution fusion | flops 22282400 | bytes 414337 | tf_op jit(solution)/shard_map/while/body/eval_jaxpr/transpose(jvp(bpsh,h->bps))/dot_general | solution.py:32
  105.7 4.3 %fusion.173 = (f32[80]{0:T(128)S(1)}, f32[4,256,80]{1,2,0:T(8,128)S(1)}, f32[4,16,80]{2,1,0:T(8,128)S(1)}) fusion(f32[4,16,80]{2,1,0:T(8,128)S(1)} %convolution_add_fusion.10, f32[4,256,80]{1,2,0:T(8,128)S(1)} %fusion.167, f32[80]{0:T(128)S(1)} %copy-done.5, f32[4,16,256]{2,1,0:T(8,128)S(1)} %convolution_multiply_fusion.3), kind=kLoop, calls=%fused_computation.20.clone.1 | loop fusion | flops 18262960 | bytes 762496 | tf_op jit(solution)/shard_map/while/body/eval_jaxpr/transpose(jvp())/reduce_sum | solution.py:30
  110.9 1.1 convolution_add_fusion.13
  112.0 1.0 convolution_add_fusion.14
  113.0 6.1 %scatter_custom_fusion.13 = f32[1024,128]{1,0:T(8,128)S(1)} fusion(s32[1024]{0:T(1024)S(1)} %bitcast.204, f32[1024,128]{1,0:T(8,128)S(1)} %bitcast.197, f32[]{:T(128)} %constant.34.clone.1..sunk), kind=kCustom, calls=%fused_computation.42.clone.1 | custom fusion | flops 131072 | bytes 524292 | tf_op jit(solution)/shard_map/while/body/eval_jaxpr/transpose(jvp())/scatter-add | solution.py:25
  119.2 0.9 fusion.178
  120.1 0.9 scatter_custom_fusion.12
  122.3 1.6 gather_fusion.1
  123.9 1.0 convolution_add_fusion.10
  124.9 3.9 %gather_fusion = f32[1024,128]{1,0:T(8,128)S(1)} fusion(f32[1024,128]{1,0:T(8,128)} %get-tuple-element.510, s32[1024]{0:T(1024)S(1)} %broadcast_clamp_fusion.2), kind=kCustom, calls=%fused_computation.clone.clone.1 | custom fusion | bytes 1052672 | tf_op jit(solution)/shard_map/while/body/eval_jaxpr/jvp()/gather | solution.py:25
  129.9 3.9 %fusion.168 = f32[1,4,16,256]{3,0,2,1:T(1,128)S(1)} fusion(f32[4,16,80]{2,1,0:T(8,128)S(1)} %convolution_add_fusion.10, f32[4,256,80]{1,2,0:T(8,128)S(1)} %fusion.167, f32[80]{0:T(128)S(1)} %copy-done.5), kind=kOutput, calls=%fused_computation.15.clone.1 | convolution fusion | flops 22282240 | bytes 414016 | tf_op jit(solution)/shard_map/while/body/eval_jaxpr/jvp(bpsh,h->bps)/dot_general | solution.py:32
  135.0 1.3 fusion.171
  138.5 4.7 %fusion.177 = f32[80]{0:T(128)S(1)} fusion(f32[4,16,80]{2,1,0:T(8,128)S(1)} %convolution_add_fusion.10, f32[4,256,80]{1,2,0:T(8,128)S(1)} %fusion.167, f32[4,16,256,1]{2,1,0,3:T(8,128)S(1)} %bitcast.199, f32[80]{0:T(128)S(1)} %get-tuple-element.480, pred[]{:T(512)S(6)} %compare.3), kind=kOutput, calls=%fused_computation.37.clone.1 | convolution fusion | flops 22282400 | bytes 414337 | tf_op jit(solution)/shard_map/while/body/eval_jaxpr/transpose(jvp(bpsh,h->bps))/dot_general | solution.py:32
  143.2 4.3 %fusion.173 = (f32[80]{0:T(128)S(1)}, f32[4,256,80]{1,2,0:T(8,128)S(1)}, f32[4,16,80]{2,1,0:T(8,128)S(1)}) fusion(f32[4,16,80]{2,1,0:T(8,128)S(1)} %convolution_add_fusion.10, f32[4,256,80]{1,2,0:T(8,128)S(1)} %fusion.167, f32[80]{0:T(128)S(1)} %copy-done.5, f32[4,16,256]{2,1,0:T(8,128)S(1)} %convolution_multiply_fusion.3), kind=kLoop, calls=%fused_computation.20.clone.1 | loop fusion | flops 18262960 | bytes 762496 | tf_op jit(solution)/shard_map/while/body/eval_jaxpr/transpose(jvp())/reduce_sum | solution.py:30
  148.5 1.1 convolution_add_fusion.13
  149.6 1.0 convolution_add_fusion.14
  150.6 6.1 %scatter_custom_fusion.13 = f32[1024,128]{1,0:T(8,128)S(1)} fusion(s32[1024]{0:T(1024)S(1)} %bitcast.204, f32[1024,128]{1,0:T(8,128)S(1)} %bitcast.197, f32[]{:T(128)} %constant.34.clone.1..sunk), kind=kCustom, calls=%fused_computation.42.clone.1 | custom fusion | flops 131072 | bytes 524292 | tf_op jit(solution)/shard_map/while/body/eval_jaxpr/transpose(jvp())/scatter-add | solution.py:25
  156.7 0.9 fusion.178
  157.6 0.9 scatter_custom_fusion.12
  159.6 10.3 %concatenate.6 = f32[283296]{0:T(1024)} concatenate(f32[131072]{0:T(1024)S(1)} %bitcast.196, f32[10240]{0:T(1024)S(1)} %reshape.162, f32[10240]{0:T(1024)S(1)} %reshape.163, f32[80]{0:T(128)S(1)} %get-tuple-element.132, f32[80]{0:T(128)S(1)} %get-tuple-element.133, f32[131072]{0:T(1024)S(1)} %bitcast.198, f32[256]{0:T(256)S(1)} %get-tuple-element.135, f32[256]{0:T(256)S(1)} %get-tuple-element.136), dimensions={0} | concatenate | bytes 2266368 | tf_op jit(solution)/shard_map/concatenate | solution.py:87
  170.0 96.1 %all-reduce.3.cloned.1.call-done = f32[283296]{0:T(1024)} async-done(((f32[283296]{0:T(1024)}), f32[283296]{0:T(1024)}) %all-reduce.3.cloned.1.call-update) | async-done | bytes 1133200 | tf_op jit(solution)/shard_map/psum | solution.py:88
  266.1 41.6 %psum.23 = f32[]{:T(128)} all-reduce(f32[]{:T(128)} %get-tuple-element.137), channel_id=1, replica_groups=mesh['batch'=16,'rep'=2] {'batch','rep'}, use_global_device_ids=true, to_apply=%region_12.13 | all-reduce | flops 1 | bytes 8 | tf_op jit(solution)/shard_map/psum | solution.py:86
  308.4 2.6 all-reduce.5.cloned.1.call-done
  310.9 2.2 slice_multiply_fusion
  313.1 0.9 div.77
  314.0 0.8 slice_multiply_fusion.2
  314.9 0.7 copy.30
  315.7 0.7 copy.29
  316.4 1.3 slice_multiply_fusion.6
  317.7 1.4 slice_multiply_fusion.4
  (173 shorter events, 23.3 us)
Async XLA Ops:
  7.2 258.9 %all-reduce.3.cloned.1.call-start = ((), (), s32[]{:S(2)}) async-start(), calls=%async_computation | async-start | bytes 2269184 | tf_op jit(solution)/shard_map/psum | solution.py:88
  12.3 4.3 %copy-start.1 = (f32[128,80]{0,1:T(8,128)S(1)}, f32[128,80]{0,1:T(8,128)}, u32[]{:S(2)}) copy-start(f32[128,80]{0,1:T(8,128)} %get-tuple-element.511) | copy-start | bytes 122884 | tf_op jit(solution)/shard_map/while
  16.2 1.1 copy-start.5
  17.2 4.3 %copy-start = (f32[512,256]{1,0:T(8,128)S(1)}, f32[512,256]{1,0:T(8,128)}, u32[]{:S(2)}) copy-start(f32[512,256]{1,0:T(8,128)} %get-tuple-element.517) | copy-start | bytes 1572868 | tf_op jit(solution)/shard_map/while
  17.3 4.3 %copy-start.4 = (f32[256]{0:T(256)S(1)}, f32[256]{0:T(256)}, u32[]{:S(2)}) copy-start(f32[256]{0:T(256)} %get-tuple-element.518) | copy-start | bytes 3076 | tf_op jit(solution)/shard_map/while
  21.2 0.8 copy-start.3
  30.6 4.8 %copy-start.2 = (f32[128,80]{0,1:T(8,128)S(1)}, f32[128,80]{0,1:T(8,128)}, u32[]{:S(2)}) copy-start(f32[128,80]{0,1:T(8,128)} %get-tuple-element.513) | copy-start | bytes 122884 | tf_op jit(solution)/shard_map/while
  49.8 4.3 %copy-start.1 = (f32[128,80]{0,1:T(8,128)S(1)}, f32[128,80]{0,1:T(8,128)}, u32[]{:S(2)}) copy-start(f32[128,80]{0,1:T(8,128)} %get-tuple-element.511) | copy-start | bytes 122884 | tf_op jit(solution)/shard_map/while
  53.7 1.1 copy-start.5
  54.8 4.3 %copy-start = (f32[512,256]{1,0:T(8,128)S(1)}, f32[512,256]{1,0:T(8,128)}, u32[]{:S(2)}) copy-start(f32[512,256]{1,0:T(8,128)} %get-tuple-element.517) | copy-start | bytes 1572868 | tf_op jit(solution)/shard_map/while
  54.8 4.3 %copy-start.4 = (f32[256]{0:T(256)S(1)}, f32[256]{0:T(256)}, u32[]{:S(2)}) copy-start(f32[256]{0:T(256)} %get-tuple-element.518) | copy-start | bytes 3076 | tf_op jit(solution)/shard_map/while
  58.7 0.8 copy-start.3
  68.1 4.8 %copy-start.2 = (f32[128,80]{0,1:T(8,128)S(1)}, f32[128,80]{0,1:T(8,128)}, u32[]{:S(2)}) copy-start(f32[128,80]{0,1:T(8,128)} %get-tuple-element.513) | copy-start | bytes 122884 | tf_op jit(solution)/shard_map/while
  87.4 4.3 %copy-start.1 = (f32[128,80]{0,1:T(8,128)S(1)}, f32[128,80]{0,1:T(8,128)}, u32[]{:S(2)}) copy-start(f32[128,80]{0,1:T(8,128)} %get-tuple-element.511) | copy-start | bytes 122884 | tf_op jit(solution)/shard_map/while
  91.2 1.1 copy-start.5
  92.3 4.3 %copy-start = (f32[512,256]{1,0:T(8,128)S(1)}, f32[512,256]{1,0:T(8,128)}, u32[]{:S(2)}) copy-start(f32[512,256]{1,0:T(8,128)} %get-tuple-element.517) | copy-start | bytes 1572868 | tf_op jit(solution)/shard_map/while
  92.3 4.3 %copy-start.4 = (f32[256]{0:T(256)S(1)}, f32[256]{0:T(256)}, u32[]{:S(2)}) copy-start(f32[256]{0:T(256)} %get-tuple-element.518) | copy-start | bytes 3076 | tf_op jit(solution)/shard_map/while
  96.3 0.8 copy-start.3
  105.6 4.8 %copy-start.2 = (f32[128,80]{0,1:T(8,128)S(1)}, f32[128,80]{0,1:T(8,128)}, u32[]{:S(2)}) copy-start(f32[128,80]{0,1:T(8,128)} %get-tuple-element.513) | copy-start | bytes 122884 | tf_op jit(solution)/shard_map/while
  124.9 4.3 %copy-start.1 = (f32[128,80]{0,1:T(8,128)S(1)}, f32[128,80]{0,1:T(8,128)}, u32[]{:S(2)}) copy-start(f32[128,80]{0,1:T(8,128)} %get-tuple-element.511) | copy-start | bytes 122884 | tf_op jit(solution)/shard_map/while
  128.8 1.1 copy-start.5
  129.9 4.3 %copy-start = (f32[512,256]{1,0:T(8,128)S(1)}, f32[512,256]{1,0:T(8,128)}, u32[]{:S(2)}) copy-start(f32[512,256]{1,0:T(8,128)} %get-tuple-element.517) | copy-start | bytes 1572868 | tf_op jit(solution)/shard_map/while
  129.9 4.3 %copy-start.4 = (f32[256]{0:T(256)S(1)}, f32[256]{0:T(256)}, u32[]{:S(2)}) copy-start(f32[256]{0:T(256)} %get-tuple-element.518) | copy-start | bytes 3076 | tf_op jit(solution)/shard_map/while
  133.8 0.8 copy-start.3
  143.2 4.8 %copy-start.2 = (f32[128,80]{0,1:T(8,128)S(1)}, f32[128,80]{0,1:T(8,128)}, u32[]{:S(2)}) copy-start(f32[128,80]{0,1:T(8,128)} %get-tuple-element.513) | copy-start | bytes 122884 | tf_op jit(solution)/shard_map/while
  169.9 141.0 %all-reduce.5.cloned.1.call-start = ((), (), s32[]{:S(2)}) async-start(), calls=%async_computation.1 | async-start | bytes 2269184 | tf_op jit(solution)/shard_map/psum | solution.py:88
Sparse Core Ops, SparseCore 0:
  170.1 95.9 all-reduce.2
  268.4 42.4 all-reduce.4
